TPU v7x, 512 devices: a whole 4x4x16 slice. The times are simulated.
512 devices in a mesh: row: 64 (over y_hi, z, core), head: 8 (over x, y_lo).
Axes of the slice: x: 4, y: 4 (y_hi: 2, y_lo: 2; y = y_hi * 2 + y_lo), z: 16, core: 2. Of those that a mesh axis runs over, the one named last changes fastest.
Arguments:
- pair_input: bfloat16 [512, 512, 128], P(('row', 'head')), may hold values from -6 to 6
- cotangent: bfloat16 [512, 512, 128], P(('row', 'head')), may hold values from -24 to 24
- residue_mask: int32 [512], replicated, may hold values from 0 to 1, as said below
- norm_gain: float32 [2, 128], replicated, may hold values from 0.5 to 1.5
- norm_shift: float32 [2, 128], replicated, may hold values from -3 to 3
- proj_weights: bfloat16 [2, 4, 128, 128], replicated, may hold values from -0.5 to 0.5
- gate_bias: float32 [2, 128], replicated, may hold values from -4 to 4
- out_weights: bfloat16 [2, 128, 128], replicated, may hold values from -1.0546875 to 1.0546875
- bias_weights: bfloat16 [2, 128, 4], replicated, may hold values from -1.06066017 to 1.06066017
Outputs:
- pair_grad: float32 [512, 512, 128], P(('row', 'head'))
- proj_grad: float32 [2, 4, 128, 128], replicated
- gate_bias_grad: float32 [2, 128], replicated
- out_grad: float32 [2, 128, 128], replicated
- bias_weight_grad: float32 [2, 128, 4], replicated
- gain_grad: float32 [2, 128], replicated
- shift_grad: float32 [2, 128], replicated
Inputs may be any that keep to these rules, and one draw needn't show every extreme that they name: `residue_mask`: 1 for the first residues of the crop and 0 for the padding after them; at least half of the 512 residues are 1.
All inputs are finite; a program needn't handle non-finite values.
Results may differ from a plain program's by a relative error of at most 0.02.
The roundings to bfloat16 on the way count: a program that leaves them out, or rounds other values in their place, can miss the bound.
Values may be sent and summed in bfloat16 or wider, within the bound.
No kernel may reach another device: no remote copies, remote signals or barrier semaphores. Data moves between devices by JAX's collectives and lax.ppermute only.
A program may use at most 64 MiB of HBM per device.

v0:
```python
import math
import jax
import jax.numpy as jnp
from jax import lax
from jax.sharding import Mesh
from jax.sharding import PartitionSpec as P

HEAD = ("head_0", "head_1")
ROW_HEAD = ("row", "head_0", "head_1")
EPS = 1e-05
MASKED = 1000000000.0


def whole_of(x, axes, dim):
    for axis in reversed(axes):
        x = lax.all_gather(x, axis, axis=dim, tiled=True)
    return x


def joined_along(parts, dim):
    parts = jnp.moveaxis(parts, 0, dim)
    dims = parts.shape
    return parts.reshape(*dims[:dim], dims[dim] * dims[dim + 1], *dims[dim + 2 :])


def from_everyone(x, axis):
    length = lax.axis_size(axis)
    return lax.all_to_all(jnp.broadcast_to(x[None], (length, *x.shape)), axis, 0, 0, tiled=True)


def gather_directly(x, axis, dim):
    return joined_along(from_everyone(x, axis), dim)


def split_up(x, dim, length):
    dims = x.shape
    parts = x.reshape(*dims[:dim], length, dims[dim] // length, *dims[dim + 1 :])
    return jnp.moveaxis(parts, dim, 0)


def sent_and_summed(x, axis, dim):
    length = lax.axis_size(axis)
    parts = lax.all_to_all(split_up(x, dim, length), axis, 0, 0, tiled=True)
    return jnp.sum(parts.astype(jnp.float32), axis=0)


def summed_on_arrival(x, axis, dim):
    parts = split_up(x, dim, lax.axis_size(axis))
    arrived = lax.all_to_all(parts, axis, split_axis=0, concat_axis=0, tiled=True)
    return arrived.sum(axis=0)


def joined_exchange(x, axis, axes, splits, concats):
    sizes = [lax.axis_size(a) for a in axes]
    parts = split_up(x, splits[0], sizes[0])
    parts = jnp.moveaxis(split_up(parts, splits[1] + 1, sizes[1]), 0, 1)
    inside = parts.shape[2:]
    parts = parts.reshape(-1, *inside)
    parts = lax.all_to_all(parts, axis, split_axis=0, concat_axis=0, tiled=True)
    parts = joined_along(parts.reshape(*sizes, *inside), concats[0] + 1)
    return joined_along(parts, concats[1])


def layer_norm(values, norm_scale, norm_offset):
    floats = values.astype(jnp.float32)
    centred = floats - jnp.mean(floats, axis=-1, keepdims=True)
    inverse = lax.rsqrt(jnp.mean(centred * centred, axis=-1, keepdims=True) + EPS)
    normed = centred * inverse
    return (normed, inverse, (normed * norm_scale + norm_offset).astype(jnp.bfloat16))


def norm_backward(grad_normal, normed, inverse, norm_scale):
    grad_hat = grad_normal * norm_scale
    first_mean = jnp.mean(grad_hat, axis=-1, keepdims=True)
    second_mean = jnp.mean(grad_hat * normed, axis=-1, keepdims=True)
    return inverse * (grad_hat - first_mean - normed * second_mean)


def class_columns(values, head_index, row_count, head_count, slab_rows):
    leading = values.shape[0]
    shaped = values.reshape(leading, row_count, head_count, slab_rows, values.shape[-1])
    picked = lax.dynamic_index_in_dim(shaped, head_index, axis=2, keepdims=False)
    return picked.reshape(leading, row_count * slab_rows, values.shape[-1])


def forward_block(pair_rows, key_bias, params, layout):
    norm_scale, norm_offset, projection, gate_offset, out_proj, bias_proj = params
    slab_rows, row_count, head_count, head_index = layout
    head_total = bias_proj.shape[1]
    inner_width = projection.shape[2]
    head_size = inner_width // head_total
    query_scale = 1.0 / math.sqrt(head_size)
    normed, inverse, normal_own = layer_norm(pair_rows, norm_scale, norm_offset)
    normal_rows = whole_of(normal_own, HEAD, 0)
    bias_own = jnp.einsum(
        "snc,ch->hsn", normal_own, bias_proj, preferred_element_type=jnp.float32
    ).astype(jnp.bfloat16)
    bias_query = gather_directly(bias_own, "row", 1)
    normal_query = class_columns(normal_rows, head_index, row_count, head_count, slab_rows)
    block_rows = normal_query.shape[0]
    query_count = normal_query.shape[1]
    key_count = normal_rows.shape[1]
    queries = (
        jnp.dot(normal_query, projection[0], preferred_element_type=jnp.float32) * query_scale
    ).astype(jnp.bfloat16)
    joined_weights = jnp.concatenate([projection[1], projection[2]], axis=1)
    key_value = jnp.dot(normal_rows, joined_weights, preferred_element_type=jnp.float32).astype(
        jnp.bfloat16
    )
    gate_values = jax.nn.sigmoid(
        jnp.dot(normal_query, projection[3], preferred_element_type=jnp.float32) + gate_offset
    )
    head_queries = queries.reshape(block_rows, query_count, head_total, head_size).transpose(
        2, 0, 1, 3
    )
    head_pairs = key_value.reshape(block_rows, key_count, 2, head_total, head_size).transpose(
        2, 3, 0, 1, 4
    )

    def attend(inputs):
        query_head, key_head, value_head, bias_head = inputs
        logits = jnp.einsum(
            "rqd,rnd->rqn", query_head, key_head, preferred_element_type=jnp.float32
        )
        logits = logits + bias_head.astype(jnp.float32)[None] + key_bias
        largest = jnp.max(logits, axis=-1, keepdims=True)
        weights = jnp.exp(logits - largest)
        total = jnp.sum(weights, axis=-1, keepdims=True)
        soft_weights = weights / total
        attended = jnp.einsum(
            "rqn,rnd->rqd",
            soft_weights.astype(jnp.bfloat16),
            value_head,
            preferred_element_type=jnp.float32,
        )
        return ((largest + jnp.log(total))[..., 0], attended)

    log_totals, attended = lax.map(attend, (head_queries, head_pairs[0], head_pairs[1], bias_query))
    attended = attended.transpose(1, 2, 0, 3).reshape(block_rows, query_count, inner_width)
    gated_out = (gate_values * attended).astype(jnp.bfloat16)
    update = jnp.dot(gated_out, out_proj, preferred_element_type=jnp.float32).astype(jnp.bfloat16)
    saved_state = (
        normed,
        inverse,
        normal_own,
        normal_rows,
        normal_query,
        head_queries,
        head_pairs,
        bias_query,
        gate_values,
        attended,
        gated_out,
        log_totals,
    )
    return (saved_state, update)


def backward_block(saved_state, grad_query, key_bias, params, layout):
    norm_scale, norm_offset, projection, gate_offset, out_proj, bias_proj = params
    slab_rows, row_count, head_count, head_index = layout
    (
        normed,
        inverse,
        normal_own,
        normal_rows,
        normal_query,
        head_queries,
        head_pairs,
        bias_query,
        gate_values,
        attended,
        gated_out,
        log_totals,
    ) = saved_state
    channels = normal_own.shape[2]
    head_total, block_rows, query_count, head_size = head_queries.shape
    key_count = normal_rows.shape[1]
    inner_width = head_total * head_size
    query_scale = 1.0 / math.sqrt(head_size)
    grad_gated = jnp.dot(grad_query, out_proj.T, preferred_element_type=jnp.float32)
    grad_att = (grad_gated * gate_values).astype(jnp.bfloat16)
    grad_pre = (grad_gated * attended * gate_values * (1.0 - gate_values)).astype(jnp.bfloat16)
    head_grads = grad_att.reshape(block_rows, query_count, head_total, head_size).transpose(
        2, 0, 1, 3
    )

    def differentiate(inputs):
        total_head, query_head, key_head, value_head, bias_head, grad_head = inputs
        logits = jnp.einsum(
            "rqd,rnd->rqn", query_head, key_head, preferred_element_type=jnp.float32
        )
        logits = logits + bias_head.astype(jnp.float32)[None] + key_bias
        soft_weights = jnp.exp(logits - total_head[..., None])
        grad_weights = jnp.einsum(
            "rqd,rnd->rqn", grad_head, value_head, preferred_element_type=jnp.float32
        )
        grad_logits = soft_weights * (
            grad_weights - jnp.sum(soft_weights * grad_weights, axis=-1, keepdims=True)
        )
        logits_half = grad_logits.astype(jnp.bfloat16)
        grad_queries = (
            jnp.einsum("rqn,rnd->rqd", logits_half, key_head, preferred_element_type=jnp.float32)
            * query_scale
        ).astype(jnp.bfloat16)
        grad_keys = jnp.einsum(
            "rqn,rqd->rnd", logits_half, query_head, preferred_element_type=jnp.float32
        ).astype(jnp.bfloat16)
        grad_values = jnp.einsum(
            "rqn,rqd->rnd",
            soft_weights.astype(jnp.bfloat16),
            grad_head,
            preferred_element_type=jnp.float32,
        ).astype(jnp.bfloat16)
        return (grad_queries, grad_keys, grad_values, jnp.sum(grad_logits, axis=0))

    grad_queries, grad_keys, grad_values, grad_bias = lax.map(
        differentiate,
        (log_totals, head_queries, head_pairs[0], head_pairs[1], bias_query, head_grads),
    )
    grad_queries = grad_queries.transpose(1, 2, 0, 3).reshape(block_rows, query_count, inner_width)
    key_weights = projection[1].reshape(channels, head_total, head_size).transpose(1, 2, 0)
    value_weights = projection[2].reshape(channels, head_total, head_size).transpose(1, 2, 0)
    query_side = jnp.dot(grad_queries, projection[0].T, preferred_element_type=jnp.float32)
    query_side = query_side + jnp.dot(grad_pre, projection[3].T, preferred_element_type=jnp.float32)
    count = slab_rows * lax.axis_size(HEAD)
    term = jnp.einsum("hrnd,hdc->rnc", grad_keys, key_weights, preferred_element_type=jnp.float32)
    term = term + jnp.einsum(
        "hrnd,hdc->rnc", grad_values, value_weights, preferred_element_type=jnp.float32
    )
    shaped = term.reshape(count, row_count, head_count, slab_rows, channels)
    current = lax.dynamic_slice_in_dim(shaped, head_index, 1, 2)
    query_slice = query_side.reshape(count, row_count, 1, slab_rows, channels)
    shaped = lax.dynamic_update_slice_in_dim(shaped, current + query_slice, head_index, 2)
    grad_normal = sent_and_summed(
        shaped.reshape(count, key_count, channels).astype(jnp.bfloat16), HEAD, 0
    )
    bias_total = summed_on_arrival(grad_bias, "row", 1)
    bias_half = bias_total.astype(jnp.bfloat16)
    grad_normal = grad_normal + jnp.einsum(
        "hsn,ch->snc", bias_half, bias_proj, preferred_element_type=jnp.float32
    )
    grad_pair = norm_backward(grad_normal, normed, inverse, norm_scale)
    projection_grads = jnp.stack(
        [
            jnp.einsum(
                "rqc,rqe->ce", normal_query, grad_queries, preferred_element_type=jnp.float32
            ),
            jnp.einsum(
                "rnc,hrnd->chd", normal_rows, grad_keys, preferred_element_type=jnp.float32
            ).reshape(channels, inner_width),
            jnp.einsum(
                "rnc,hrnd->chd", normal_rows, grad_values, preferred_element_type=jnp.float32
            ).reshape(channels, inner_width),
            jnp.einsum("rqc,rqe->ce", normal_query, grad_pre, preferred_element_type=jnp.float32),
        ]
    )
    weight_grads = (
        projection_grads,
        jnp.sum(grad_pre.astype(jnp.float32), axis=(0, 1)),
        jnp.einsum("rqe,rqc->ec", gated_out, grad_query, preferred_element_type=jnp.float32),
        jnp.einsum("snc,hsn->ch", normal_own, bias_half, preferred_element_type=jnp.float32),
        jnp.sum(grad_normal * normed, axis=(0, 1)),
        jnp.sum(grad_normal, axis=(0, 1)),
    )
    return (grad_pair, weight_grads)


def to_queries(grad_rows, layout):
    slab_rows, row_count, head_count, head_index = layout
    channels = grad_rows.shape[2]
    shaped = grad_rows.reshape(slab_rows, row_count, head_count, slab_rows, channels)
    moved = lax.all_to_all(shaped, HEAD, split_axis=2, concat_axis=0, tiled=True)
    return moved.reshape(slab_rows * head_count, row_count * slab_rows, channels)


def local(
    pair_input,
    cotangent,
    residue_mask,
    norm_gain,
    norm_shift,
    proj_weights,
    gate_bias,
    out_weights,
    bias_weights,
):
    slab_rows = pair_input.shape[0]
    channels = pair_input.shape[2]
    row_count = lax.axis_size("row")
    head_count = lax.axis_size(HEAD)
    layout = (slab_rows, row_count, head_count, lax.axis_index(HEAD))
    key_bias = (residue_mask.astype(jnp.float32) - 1.0) * MASKED
    params = [
        (
            norm_gain[which],
            norm_shift[which],
            proj_weights[which],
            gate_bias[which],
            out_weights[which],
            bias_weights[which],
        )
        for which in range(2)
    ]
    first_state, first_update = forward_block(pair_input, key_bias, params[0], layout)
    returned = lax.all_to_all(
        first_update.reshape(slab_rows * head_count, row_count, 1, slab_rows, channels),
        HEAD,
        split_axis=0,
        concat_axis=2,
        tiled=True,
    )
    after_first = (
        pair_input.astype(jnp.float32)
        + returned.reshape(slab_rows, -1, channels).astype(jnp.float32)
    ).astype(jnp.bfloat16)
    joined = jnp.concatenate([after_first, cotangent], axis=2)
    moved = joined_exchange(
        joined.reshape(1, 1, slab_rows, row_count, head_count, slab_rows, 2 * channels),
        ROW_HEAD,
        ("row", HEAD),
        (3, 4),
        (0, 1),
    )
    flipped = moved.reshape(-1, slab_rows, 2 * channels).transpose(1, 0, 2)
    second_state, second_update = forward_block(
        flipped[:, :, :channels], key_bias, params[1], layout
    )
    second_grad, second_weights = backward_block(
        second_state, to_queries(flipped[:, :, channels:], layout), key_bias, params[1], layout
    )
    sent_back = joined_exchange(
        second_grad.astype(jnp.bfloat16).reshape(
            1, 1, slab_rows, row_count, head_count, slab_rows, channels
        ),
        ROW_HEAD,
        ("row", HEAD),
        (3, 4),
        (0, 1),
    )
    end_grad = sent_back.reshape(-1, slab_rows, channels).transpose(1, 0, 2)
    grad_after = cotangent.astype(jnp.float32) + end_grad.astype(jnp.float32)
    start_grad, first_weights = backward_block(
        first_state,
        to_queries(grad_after.astype(jnp.bfloat16), layout),
        key_bias,
        params[0],
        layout,
    )
    pair_grad = grad_after + start_grad
    combined = [
        jnp.stack([start_part, end_part])
        for start_part, end_part in zip(first_weights, second_weights)
    ]
    stacked = lax.psum(
        (combined[0], combined[1], combined[2], combined[3], combined[4], combined[5]), ROW_HEAD
    )
    return (pair_grad, stacked[0], stacked[1], stacked[2], stacked[3], stacked[4], stacked[5])


def solution(mesh):
    finer = Mesh(mesh.devices.reshape(mesh.shape["row"], 4, 2), ("row", "head_0", "head_1"))
    in_specs = (P(ROW_HEAD, None, None), P(ROW_HEAD, None, None), P(), P(), P(), P(), P(), P(), P())
    out_specs = (P(ROW_HEAD, None, None), P(), P(), P(), P(), P(), P())
    return jax.shard_map(local, mesh=finer, in_specs=in_specs, out_specs=out_specs, check_vma=False)
```

profile of v0, /device:TPU:1, one launch (start us, length us, event | category | flops | bytes accessed | tf_op | source)
XLA Modules:
  0.0 951.6 jit_solution(1266465462356417426)
XLA Ops:
  11.9 5.2 all_gather.12
  18.7 20.5 %all-to-all-start = ((bf16[64,4,1,512]{3,1,2,0:T(4,128)(2,1)}), bf16[64,4,1,512]{3,1,2,0:T(4,128)(2,1)S(1)}, u32[]{:S(2)}, u32[]{:S(2)}) async-start(bf16[64,4,1,512]{3,1,2,0:T(4,128)(2,1)} %broadcast_in_dim.57), calls=%async_computation | async-start | bytes 524288 | tf_op jit(solution)/shard_map/all_to_all | solution.py:28
  40.8 22.2 %all-to-all-done = bf16[64,4,1,512]{3,1,2,0:T(4,128)(2,1)S(1)} async-done(((bf16[64,4,1,512]{3,1,2,0:T(4,128)(2,1)}), bf16[64,4,1,512]{3,1,2,0:T(4,128)(2,1)S(1)}, u32[]{:S(2)}, u32[]{:S(2)}) %all-to-all-start) | async-done | bytes 262176 | tf_op jit(solution)/shard_map/all_to_all | solution.py:28
  68.0 11.2 %while.56 = (s32[]{:T(128)}, f32[4,8,64]{2,1,0:T(8,128)}, f32[4,8,64,32]{2,3,1,0:T(8,128)S(1)}, bf16[4,8,64,32]{2,3,1,0:T(8,128)(2,1)S(1)}, bf16[4,8,512,32]{2,3...) while((s32[]{:T(128)}, f32[4,8,64]{2,1,0:T(8,128)}, ...), condition=%wide.region_5.6_spmd, body=%wide.region_2.5_spmd.sunk | while | flops 35683840 | bytes 4221537 | solution.py:138
  81.3 9.2 all_to_all.79
  92.2 36.4 %all_to_all.80 = bf16[512,2,128]{2,1,0:T(2,128)(2,1)S(1)} all-to-all(bf16[512,2,128]{2,1,0:T(2,128)(2,1)S(1)} %reshape.464), channel_id=1, replica_groups=mesh['row'=64,'head_0'=4,'head_1'=2] {'row','head_0','head_1'}, dimensions={0} | all-to-all | bytes 524288 | tf_op jit(solution)/shard_map/all_to_all | solution.py:59
  129.4 6.0 all_gather.14
  139.6 5.0 all-to-all-done.4
  145.4 6.2 all-to-all-start.3
  152.1 23.3 %all-to-all-done.3 = bf16[64,4,1,512]{3,1,2,0:T(4,128)(2,1)S(1)} async-done(((bf16[64,4,1,512]{3,1,2,0:T(4,128)(2,1)}), bf16[64,4,1,512]{3,1,2,0:T(4,128)(2,1)S(1)}, u32[]{:S(2)}, u32[]{:S(2)}) %all-to-all-start.3) | async-done | bytes 262176 | tf_op jit(solution)/shard_map/all_to_all | solution.py:28
  182.5 18.3 %while.57 = (s32[]{:T(128)}, f32[4,8,64]{2,1,0:T(8,128)}, f32[4,8,64,32]{2,3,1,0:T(8,128)S(1)}, bf16[4,8,64,32]{2,3,1,0:T(8,128)(2,1)S(1)}, bf16[4,8,512,32]{2,3...) while((s32[]{:T(128)}, f32[4,8,64]{2,1,0:T(8,128)}, ...), condition=%wide.region_11.12_spmd, body=%wide.region_8.11_spmd.sunk | while | flops 35683840 | bytes 4221537 | solution.py:138
  207.3 51.8 %while.58 = (s32[]{:T(128)}, bf16[4,8,64,32]{2,3,1,0:T(8,128)(2,1)}, bf16[4,8,512,32]{2,3,1,0:T(8,128)(2,1)}, bf16[4,8,512,32]{2,3,1,0:T(8,128)(2,1)}, f32[4,64,...) while((s32[]{:T(128)}, ...), condition=%wide.region_15.16_spmd, body=%wide.region_12.15_spmd.sunk | while | flops 86801920 | bytes 10505361 | solution.py:217
  264.6 6.1 dynamic_update_slice.47
  270.9 18.0 %all_to_all.81 = bf16[8,1,512,128]{3,2,1,0:T(8,128)(2,1)S(1)} all-to-all(bf16[8,1,512,128]{3,2,1,0:T(8,128)(2,1)S(1)} %convert_bitcast_fusion.1), channel_id=1, replica_groups=mesh['row'=64,'head_0'=4,'head_1'=2] {'head_0','head_1'}, dimensions={0} | all-to-all | bytes 2097152 | tf_op jit(solution)/shard_map/all_to_all | solution.py:43
  294.4 32.6 %all-to-all-done.6 = f32[64,4,1,512]{3,1,2,0:T(4,128)S(1)} async-done(((f32[64,4,1,512]{3,1,2,0:T(4,128)}), f32[64,4,1,512]{3,1,2,0:T(4,128)S(1)}, u32[]{:S(2)}, u32[]{:S(2)}) %all-to-all-start.6) | async-done | bytes 524320 | tf_op jit(solution)/shard_map/all_to_all | solution.py:49
  331.6 9.3 all-to-all-start.7
  340.9 24.7 %all-to-all-done.7 = bf16[512,1,1,1,1,1,1,128]{7,6,5,4,3,2,1,0:T(2,128)(2,1)S(1)} async-done(((bf16[512,1,1,1,1,1,1,128]{7,6,5,4,3,2,1,0:T(2,128)(2,1)}), bf16[512,1,1,1,1,1,1,128]{7,6,5,4,3,2,1,0:T(2,128)(2,1)S(1)}, u32[]{:S(2)}, u32[]{:S(2)}) %all-to-all-start.7) | async-done | bytes 131104 | tf_op jit(solution)/shard_map/all_to_all | solution.py:59
  381.1 40.7 %while.59 = (s32[]{:T(128)}, bf16[4,8,64,32]{2,3,1,0:T(8,128)(2,1)}, bf16[4,8,512,32]{2,3,1,0:T(8,128)(2,1)}, bf16[4,8,512,32]{2,3,1,0:T(8,128)(2,1)}, f32[4,64,...) while((s32[]{:T(128)}, ...), condition=%wide.region_23.24_spmd, body=%wide.region_20.23_spmd.sunk | while | flops 86801920 | bytes 10505361 | solution.py:217
  427.3 6.1 dynamic_update_slice.48
  447.7 5.1 all-to-all-done.9
  452.8 6.7 all-to-all-start.10
  470.6 22.2 %all-to-all-done.10 = f32[64,4,1,512]{3,1,2,0:T(4,128)} async-done(((f32[64,4,1,512]{3,1,2,0:T(4,128)}), f32[64,4,1,512]{3,1,2,0:T(4,128)}, u32[]{:S(2)}, u32[]{:S(2)}) %all-to-all-start.10) | async-done | bytes 524320 | tf_op jit(solution)/shard_map/all_to_all | solution.py:49
  494.8 100.0 %all-reduce = (f32[2,128]{1,0:T(2,128)}, f32[2,128,4]{1,2,0:T(4,128)}, f32[2,128]{1,0:T(2,128)}, f32[2,128]{1,0:T(2,128)}) all-reduce(f32[2,128]{1,0:T(2,128)S(1)} %pad_maximum_fusion.3, f32[2,128,4]{1,2,0:T(4,128)S(1)} %pad_maximum_fusion.2, ...), channel_id=1, replica_groups=mesh['row'=64,'head_0'=4,'head_1'=2] {'row','head_0','head_1'}, use_global_device_ids=true, to_apply=%region_31.32 | all-reduce | flops 1792 | bytes 14336 | tf_op jit(solution)/shard_map/psum | solution.py:355
  595.8 345.8 %all-reduce.4.cloned.1.call-done = (f32[2,4,128,128]{3,2,1,0:T(8,128)}, f32[2,128,128]{2,1,0:T(8,128)}) async-done(((f32[2,4,128,128]{3,2,1,0:T(8,128)}, f32[2,128,128]{2,1,0:T(8,128)}), (f32[2,4,128,128]{3,2,1,0:T(8,128)}, f32[2,128,128]{2,1,0:T(8,128)})) %all-reduce.4.cloned.1.call-update) | async-done | bytes 655376 | tf_op jit(solution)/shard_map/psum | solution.py:355
  (406 shorter events, 225.8 us)
Async XLA Ops:
  7.2 55.9 %all-gather.3.cloned.1.call-start = ((), (), s32[]{:S(2)}) async-start(), calls=%async_computation.11 | async-start | bytes 1310720 | tf_op jit(solution)/shard_map/all_gather | solution.py:16
  10.7 118.4 %copy-start.59 = (f32[128]{0:T(128)}, f32[128]{0:T(128)S(1)}, u32[]{:S(2)}) copy-start(f32[128]{0:T(128)S(1)} %get-tuple-element.487) | copy-start | bytes 1540
  11.9 53.3 %copy-start.18 = (bf16[1,512,128]{2,1,0:T(8,128)(2,1)}, bf16[1,512,128]{2,1,0:T(8,128)(2,1)S(1)}, u32[]{:S(2)}) copy-start(bf16[1,512,128]{2,1,0:T(8,128)(2,1)S(1)} %fusion.128) | copy-start | bytes 393220
  18.7 44.3 %all-to-all-start = ((bf16[64,4,1,512]{3,1,2,0:T(4,128)(2,1)}), bf16[64,4,1,512]{3,1,2,0:T(4,128)(2,1)S(1)}, u32[]{:S(2)}, u32[]{:S(2)}) async-start(bf16[64,4,1,512]{3,1,2,0:T(4,128)(2,1)} %broadcast_in_dim.57), calls=%async_computation | async-start | bytes 524288 | tf_op jit(solution)/shard_map/all_to_all | solution.py:28
  39.3 136.8 %all-gather.5.cloned.1.call-start = ((), (), s32[]{:S(2)}) async-start(), calls=%async_computation.12 | async-start | bytes 1310720 | tf_op jit(solution)/shard_map/all_gather | solution.py:16
  128.7 49.3 %copy-start.6 = (bf16[512,1,1,1,1,1,1,256]{7,0,5,4,3,2,1,6:T(8,128)(2,1)}, bf16[512,1,1,1,1,1,1,256]{7,0,5,4,3,2,1,6:T(8,128)(2,1)S(1)}, u32[]{:S(2)}) copy-start(bf16[512,1,1,1,1,1,1,256]{7,0,5,4,3,2,1,6:T(8,128)(2,1)S(1)} %copy.243) | copy-start | bytes 786436
  129.4 48.7 %copy-start.20 = (bf16[1,512,128]{2,1,0:T(8,128)(2,1)}, bf16[1,512,128]{2,1,0:T(8,128)(2,1)S(1)}, u32[]{:S(2)}) copy-start(bf16[1,512,128]{2,1,0:T(8,128)(2,1)S(1)} %fusion.136) | copy-start | bytes 393220
  136.1 8.6 all-to-all-start.4
  145.4 29.9 %all-to-all-start.3 = ((bf16[64,4,1,512]{3,1,2,0:T(4,128)(2,1)}), bf16[64,4,1,512]{3,1,2,0:T(4,128)(2,1)S(1)}, u32[]{:S(2)}, u32[]{:S(2)}) async-start(bf16[64,4,1,512]{3,1,2,0:T(4,128)(2,1)} %broadcast_in_dim.74), calls=%async_computation.3 | async-start | bytes 524288 | tf_op jit(solution)/shard_map/all_to_all | solution.py:28
  207.3 51.8 %copy-start.45 = (bf16[1,1,128,128]{2,3,1,0:T(8,128)(2,1)S(1)}, bf16[1,1,128,128]{2,3,1,0:T(8,128)(2,1)}, u32[]{:S(2)}) copy-start(bf16[1,1,128,128]{2,3,1,0:T(8,128)(2,1)} %copy-done.44) | copy-start | bytes 98308
  270.8 56.3 %copy-start.7 = (bf16[512,1,1,1,1,1,1,256]{7,0,5,4,3,2,1,6:T(8,128)(2,1)S(1)}, bf16[512,1,1,1,1,1,1,256]{7,0,5,4,3,2,1,6:T(8,128)(2,1)}, u32[]{:S(2)}) copy-start(bf16[512,1,1,1,1,1,1,256]{7,0,5,4,3,2,1,6:T(8,128)(2,1)} %copy-done.6) | copy-start | bytes 786436
  270.8 56.3 %copy-start.56 = (f32[512]{0:T(512)S(1)}, f32[512]{0:T(512)}, u32[]{:S(2)}) copy-start(f32[512]{0:T(512)} %copy-done.55) | copy-start | bytes 6148
  270.8 56.3 %copy-start.60 = (f32[128]{0:T(128)S(1)}, f32[128]{0:T(128)}, u32[]{:S(2)}) copy-start(f32[128]{0:T(128)} %copy-done.59) | copy-start | bytes 1540
  270.9 56.3 %copy-start.62 = (bf16[2,128,4]{1,2,0:T(4,128)(2,1)S(1)}, bf16[2,128,4]{1,2,0:T(4,128)(2,1)}, u32[]{:S(2)}) copy-start(bf16[2,128,4]{1,2,0:T(4,128)(2,1)} %param.25) | copy-start | bytes 6148
  288.8 38.1 %all-to-all-start.6 = ((f32[64,4,1,512]{3,1,2,0:T(4,128)}), f32[64,4,1,512]{3,1,2,0:T(4,128)S(1)}, u32[]{:S(2)}, u32[]{:S(2)}) async-start(f32[64,4,1,512]{3,1,2,0:T(4,128)} %bitcast.128), calls=%async_computation.6 | async-start | bytes 1048576 | tf_op jit(solution)/shard_map/all_to_all | solution.py:49
  293.5 73.0 %copy-start.29 = (bf16[1,512,128]{2,1,0:T(8,128)(2,1)S(1)}, bf16[1,512,128]{2,1,0:T(8,128)(2,1)}, u32[]{:S(2)}) copy-start(bf16[1,512,128]{2,1,0:T(8,128)(2,1)} %param.18) | copy-start | bytes 393220
  331.6 33.9 %all-to-all-start.7 = ((bf16[512,1,1,1,1,1,1,128]{7,6,5,4,3,2,1,0:T(2,128)(2,1)}), bf16[512,1,1,1,1,1,1,128]{7,6,5,4,3,2,1,0:T(2,128)(2,1)S(1)}, u32[]{:S(2)}, u32[]{:S(2)}) async-start(bf16[512,1,1,1,1,1,1,128]{7,6,5,4,3,2,1,0:T(2,128)(2,1)} %copy.171), calls=%async_computation.7 | async-start | bytes 524288 | tf_op jit(solution)/shard_map/all_to_all | solution.py:59
  367.2 8.6 all-to-all-start.8
  377.0 48.6 %copy-start.26 = (bf16[8,64,128]{2,1,0:T(8,128)(2,1)}, bf16[8,64,128]{2,1,0:T(8,128)(2,1)S(1)}, u32[]{:S(2)}) copy-start(bf16[8,64,128]{2,1,0:T(8,128)(2,1)S(1)} %get-tuple-element.450) | copy-start | bytes 393220
  434.5 18.3 %all-to-all-start.9 = ((bf16[8,1,512,128]{3,2,1,0:T(8,128)(2,1)}), bf16[8,1,512,128]{3,2,1,0:T(8,128)(2,1)S(1)}, u32[]{:S(2)}, u32[]{:S(2)}) async-start(bf16[8,1,512,128]{3,2,1,0:T(8,128)(2,1)} %convert_bitcast_fusion), calls=%async_computation.9 | async-start | bytes 2097152 | tf_op jit(solution)/shard_map/all_to_all | solution.py:43
  452.8 40.0 %all-to-all-start.10 = ((f32[64,4,1,512]{3,1,2,0:T(4,128)}), f32[64,4,1,512]{3,1,2,0:T(4,128)}, u32[]{:S(2)}, u32[]{:S(2)}) async-start(f32[64,4,1,512]{3,1,2,0:T(4,128)} %bitcast.624), calls=%async_computation.10 | async-start | bytes 1048576 | tf_op jit(solution)/shard_map/all_to_all | solution.py:49
  459.5 482.1 %all-reduce.4.cloned.1.call-start = ((), (), s32[]{:S(2)}) async-start(), calls=%async_computation.13 | async-start | bytes 1310720 | tf_op jit(solution)/shard_map/psum | solution.py:355
  469.6 125.2 %copy-start.14 = (f32[512,1,1,1,1,1,1,128]{7,6,5,4,3,2,1,0:T(1,128)S(1)}, f32[512,1,1,1,1,1,1,128]{7,6,5,4,3,2,1,0:T(1,128)}, u32[]{:S(2)}) copy-start(f32[512,1,1,1,1,1,1,128]{7,6,5,4,3,2,1,0:T(1,128)} %copy-done.13) | copy-start | bytes 786436
  469.6 125.2 %copy-start.30 = (bf16[1,512,128]{2,1,0:T(8,128)(2,1)S(1)}, bf16[1,512,128]{2,1,0:T(8,128)(2,1)}, u32[]{:S(2)}) copy-start(bf16[1,512,128]{2,1,0:T(8,128)(2,1)} %param.18) | copy-start | bytes 393220
  (58 other events, 965.1 us)
Sparse Core Ops, SparseCore 0:
  17.2 35.9 all-gather.2
  135.5 18.4 all-gather.4
  470.6 471.0 all-reduce.3
where the time goes:
time: 957 us; the launch traced here: 952 us
  waiting for transfers between devices  484 us (51%)
  blocking collectives  175 us (18%)
  matrix products  101 us (11%)
  local copies, waits for them, and re-layouts  82.8 us (9%)
  starting transfers between devices  57.9 us (6%)
  other arithmetic  35.6 us (4%)
  between operations  15 us (2%)
    psum x1, waiting for transfers between devices, local(): lax.psum((combined[0], combined[1], combined[2], combined[3], combined[4]...  346 us
    psum x1, blocking collectives, local(): lax.psum((combined[0], combined[1], combined[2], combined[3], combined[4]...  100 us
    all_to_all x2, waiting for transfers between devices, summed_on_arrival(): lax.all_to_all(parts, axis, split_axis=0, concat_axis=0, tiled=True)  54.8 us
    all_to_all x2, waiting for transfers between devices, from_everyone(): lax.all_to_all(jnp.broadcast_to(x[None], (length, *x.shape)), axis, 0, 0,...  45.5 us
    all_to_all x1, blocking collectives, joined_exchange(): parts = lax.all_to_all(parts, axis, split_axis=0, concat_axis=0, tiled=True)  36.4 us
    dynamic_update_slice x16, local copies, waits for them, and re-layouts, backward_block(): lax.map(differentiate, (log_totals, head_queries, head_pairs[0], head_pai...  30.2 us
    all_to_all x2, starting transfers between devices, from_everyone(): lax.all_to_all(jnp.broadcast_to(x[None], (length, *x.shape)), axis, 0, 0,...  26.7 us
    all_to_all x1, waiting for transfers between devices, joined_exchange(): parts = lax.all_to_all(parts, axis, split_axis=0, concat_axis=0, tiled=True)  24.7 us
  transfers between devices with their start and end apart: 11, of which 9 were waited for; matrix products, arithmetic and copies ran while one was open for 3% of the time, Pallas kernels for 0%

commit v1 on v0

--- a/solution.py
+++ b/solution.py
@@ -352,9 +352,11 @@
         jnp.stack([start_part, end_part])
         for start_part, end_part in zip(first_weights, second_weights)
     ]
-    stacked = lax.psum(
-        (combined[0], combined[1], combined[2], combined[3], combined[4], combined[5]), ROW_HEAD
-    )
+    one_axis = lax.psum(
+        (combined[0], combined[1], combined[2], combined[3], combined[4], combined[5]),
+        ("head_0", "head_1"),
+    )
+    stacked = lax.psum(one_axis, "row")
     return (pair_grad, stacked[0], stacked[1], stacked[2], stacked[3], stacked[4], stacked[5])
 
 

time: 957 us -> 1070 us (1.12)
  blocking collectives: 175 us -> 230 us
  waiting for transfers between devices: 484 us -> 537 us
    psum x0 -> x1, waiting for transfers between devices: none -> 344 us  [local(): stacked = lax.psum(one_axis, 'row')]
    psum x1, waiting for transfers between devices: 346 us -> 84.5 us  [local(): lax.psum((combined[0], combined[1], combined[2], combined[3], combined[4]...]
    psum x0 -> x1, blocking collectives: none -> 142 us  [local(): stacked = lax.psum(one_axis, 'row')]
    psum x1, blocking collectives: 100 us -> 13.4 us  [local(): lax.psum((combined[0], combined[1], combined[2], combined[3], combined[4]...]
    all_to_all x2, waiting for transfers between devices: 54.8 us -> 32.5 us  [summed_on_arrival(): lax.all_to_all(parts, axis, split_axis=0, concat_axis=0, tiled=True)]
  transfers between devices with their start and end apart: 11 -> 12, of which waited for: 9 -> 9; matrix products, arithmetic and copies ran while one was open for 3% -> 3% of each run, Pallas kernels for 0% -> 0%
where the time goes in v1:
time: 1070 us
  waiting for transfers between devices  537 us (50%)
  blocking collectives  230 us (21%)
  matrix products  102 us (10%)
  local copies, waits for them, and re-layouts  83.2 us (8%)
  starting transfers between devices  61 us (6%)
  other arithmetic  36.9 us (3%)
  between operations  15 us (1%)
    psum x1, waiting for transfers between devices, local(): stacked = lax.psum(one_axis, 'row')  344 us
    psum x1, blocking collectives, local(): stacked = lax.psum(one_axis, 'row')  142 us
    psum x1, waiting for transfers between devices, local(): lax.psum((combined[0], combined[1], combined[2], combined[3], combined[4]...  84.5 us
    all_to_all x2, waiting for transfers between devices, from_everyone(): lax.all_to_all(jnp.broadcast_to(x[None], (length, *x.shape)), axis, 0, 0,...  45.5 us
    all_to_all x1, blocking collectives, joined_exchange(): parts = lax.all_to_all(parts, axis, split_axis=0, concat_axis=0, tiled=True)  36.4 us
    all_to_all x2, waiting for transfers between devices, summed_on_arrival(): lax.all_to_all(parts, axis, split_axis=0, concat_axis=0, tiled=True)  32.5 us
    dynamic_update_slice x16, local copies, waits for them, and re-layouts, backward_block(): lax.map(differentiate, (log_totals, head_queries, head_pairs[0], head_pai...  30.2 us
    all_to_all x2, starting transfers between devices, from_everyone(): lax.all_to_all(jnp.broadcast_to(x[None], (length, *x.shape)), axis, 0, 0,...  26.7 us
  transfers between devices with their start and end apart: 12, of which 9 were waited for; matrix products, arithmetic and copies ran while one was open for 3% of the time, Pallas kernels for 0%

profile of v1, /device:TPU:1, one launch (start us, length us, event | category | flops | bytes accessed | tf_op | source)
XLA Modules:
  0.0 1065.5 jit_solution(5062274587073686059)
XLA Ops:
  12.4 5.2 all_gather.12
  19.2 20.5 %all-to-all-start = ((bf16[64,4,1,512]{3,1,2,0:T(4,128)(2,1)}), bf16[64,4,1,512]{3,1,2,0:T(4,128)(2,1)S(1)}, u32[]{:S(2)}, u32[]{:S(2)}) async-start(bf16[64,4,1,512]{3,1,2,0:T(4,128)(2,1)} %broadcast_in_dim.57), calls=%async_computation | async-start | bytes 524288 | tf_op jit(solution)/shard_map/all_to_all | solution.py:28
  41.3 22.2 %all-to-all-done = bf16[64,4,1,512]{3,1,2,0:T(4,128)(2,1)S(1)} async-done(((bf16[64,4,1,512]{3,1,2,0:T(4,128)(2,1)}), bf16[64,4,1,512]{3,1,2,0:T(4,128)(2,1)S(1)}, u32[]{:S(2)}, u32[]{:S(2)}) %all-to-all-start) | async-done | bytes 262176 | tf_op jit(solution)/shard_map/all_to_all | solution.py:28
  67.9 8.9 while.56
  79.5 9.2 all_to_all.79
  90.4 36.4 %all_to_all.80 = bf16[512,2,128]{2,1,0:T(2,128)(2,1)S(1)} all-to-all(bf16[512,2,128]{2,1,0:T(2,128)(2,1)S(1)} %reshape.464), channel_id=1, replica_groups=mesh['row'=64,'head_0'=4,'head_1'=2] {'row','head_0','head_1'}, dimensions={0} | all-to-all | bytes 524288 | tf_op jit(solution)/shard_map/all_to_all | solution.py:59
  127.6 6.0 all_gather.14
  143.7 6.2 all-to-all-start.3
  150.3 23.3 %all-to-all-done.3 = bf16[64,4,1,512]{3,1,2,0:T(4,128)(2,1)S(1)} async-done(((bf16[64,4,1,512]{3,1,2,0:T(4,128)(2,1)}), bf16[64,4,1,512]{3,1,2,0:T(4,128)(2,1)S(1)}, u32[]{:S(2)}, u32[]{:S(2)}) %all-to-all-start.3) | async-done | bytes 262176 | tf_op jit(solution)/shard_map/all_to_all | solution.py:28
  180.8 18.3 %while.57 = (s32[]{:T(128)}, f32[4,8,64]{2,1,0:T(8,128)}, f32[4,8,64,32]{2,3,1,0:T(8,128)S(1)}, bf16[4,8,64,32]{2,3,1,0:T(8,128)(2,1)S(1)}, bf16[4,8,512,32]{2,3...) while((s32[]{:T(128)}, f32[4,8,64]{2,1,0:T(8,128)}, ...), condition=%wide.region_11.12_spmd, body=%wide.region_8.11_spmd.sunk | while | flops 35683840 | bytes 4221537 | solution.py:138
  205.5 51.8 %while.58 = (s32[]{:T(128)}, bf16[4,8,64,32]{2,3,1,0:T(8,128)(2,1)}, bf16[4,8,512,32]{2,3,1,0:T(8,128)(2,1)}, bf16[4,8,512,32]{2,3,1,0:T(8,128)(2,1)}, f32[4,64,...) while((s32[]{:T(128)}, ...), condition=%wide.region_15.16_spmd, body=%wide.region_12.15_spmd.sunk | while | flops 86801920 | bytes 10505361 | solution.py:217
  262.8 6.1 dynamic_update_slice.47
  269.1 17.9 %all_to_all.81 = bf16[8,1,512,128]{3,2,1,0:T(8,128)(2,1)S(1)} all-to-all(bf16[8,1,512,128]{3,2,1,0:T(8,128)(2,1)S(1)} %convert_bitcast_fusion.1), channel_id=1, replica_groups=mesh['row'=64,'head_0'=4,'head_1'=2] {'head_0','head_1'}, dimensions={0} | all-to-all | bytes 2097152 | tf_op jit(solution)/shard_map/all_to_all | solution.py:43
  287.0 5.5 all-to-all-start.6
  293.3 32.5 %all-to-all-done.6 = f32[64,4,1,512]{3,1,2,0:T(4,128)} async-done(((f32[64,4,1,512]{3,1,2,0:T(4,128)}), f32[64,4,1,512]{3,1,2,0:T(4,128)}, u32[]{:S(2)}, u32[]{:S(2)}) %all-to-all-start.6) | async-done | bytes 524320 | tf_op jit(solution)/shard_map/all_to_all | solution.py:49
  332.4 11.3 %all-to-all-start.7 = ((bf16[512,1,1,1,1,1,1,128]{7,6,5,4,3,2,1,0:T(2,128)(2,1)}), bf16[512,1,1,1,1,1,1,128]{7,6,5,4,3,2,1,0:T(2,128)(2,1)}, u32[]{:S(2)}, u32[]{:S(2)}) async-start(bf16[512,1,1,1,1,1,1,128]{7,6,5,4,3,2,1,0:T(2,128)(2,1)} %copy.171), calls=%async_computation.7 | async-start | bytes 524288 | tf_op jit(solution)/shard_map/all_to_all | solution.py:59
  346.1 20.1 %all-to-all-done.7 = bf16[512,1,1,1,1,1,1,128]{7,6,5,4,3,2,1,0:T(2,128)(2,1)} async-done(((bf16[512,1,1,1,1,1,1,128]{7,6,5,4,3,2,1,0:T(2,128)(2,1)}), bf16[512,1,1,1,1,1,1,128]{7,6,5,4,3,2,1,0:T(2,128)(2,1)}, u32[]{:S(2)}, u32[]{:S(2)}) %all-to-all-start.7) | async-done | bytes 131104 | tf_op jit(solution)/shard_map/all_to_all | solution.py:59
  383.3 40.7 %while.59 = (s32[]{:T(128)}, bf16[4,8,64,32]{2,3,1,0:T(8,128)(2,1)}, bf16[4,8,512,32]{2,3,1,0:T(8,128)(2,1)}, bf16[4,8,512,32]{2,3,1,0:T(8,128)(2,1)}, f32[4,64,...) while((s32[]{:T(128)}, ...), condition=%wide.region_23.24_spmd, body=%wide.region_20.23_spmd.sunk | while | flops 86801920 | bytes 10505361 | solution.py:217
  429.4 6.1 dynamic_update_slice.48
  454.8 6.9 all-to-all-start.10
  469.3 84.5 %all-reduce.9.cloned.1.call-done = (f32[2,4,128,128]{3,2,1,0:T(8,128)}, f32[2,128,128]{2,1,0:T(8,128)}) async-done(((f32[2,4,128,128]{3,2,1,0:T(8,128)}, f32[2,128,128]{2,1,0:T(8,128)}), (f32[2,4,128,128]{3,2,1,0:T(8,128)}, f32[2,128,128]{2,1,0:T(8,128)})) %all-reduce.9.cloned.1.call-update) | async-done | bytes 655376 | tf_op jit(solution)/shard_map/psum | solution.py:355
  554.9 13.4 %all-reduce.2 = (f32[2,128]{1,0:T(2,128)S(1)}, f32[2,128,4]{1,2,0:T(4,128)S(1)}, f32[2,128]{1,0:T(2,128)S(1)}, f32[2,128]{1,0:T(2,128)S(1)}) all-reduce(f32[2,128]{1,0:T(2,128)S(1)} %pad_maximum_fusion.3, f32[2,128,4]{1,2,0:T(4,128)S(1)} %pad_maximum_fusion.2, ...), channel_id=1, replica_groups=mesh['row'=64,'head_0'=4,'head_1'=2] {'head_0','head_1'}, use_global_device_ids=true, to_apply=%region_32.33 | all-reduce | flops 1792 | bytes 14336 | tf_op jit(solution)/shard_map/psum | solution.py:355
  568.3 141.9 %all-reduce = (f32[2,128]{1,0:T(2,128)}, f32[2,128,4]{1,2,0:T(4,128)}, f32[2,128]{1,0:T(2,128)}, f32[2,128]{1,0:T(2,128)}) all-reduce(f32[2,128]{1,0:T(2,128)S(1)} %get-tuple-element.449, f32[2,128,4]{1,2,0:T(4,128)S(1)} %get-tuple-element.450, ...), channel_id=1, replica_groups=mesh['row'=64,'head_0'=4,'head_1'=2] {'row'}, use_global_device_ids=true, to_apply=%region_33.34 | all-reduce | flops 1792 | bytes 14336 | tf_op jit(solution)/shard_map/psum | solution.py:359
  711.3 344.3 %all-reduce.7.cloned.1.call-done = (f32[2,4,128,128]{3,2,1,0:T(8,128)}, f32[2,128,128]{2,1,0:T(8,128)}) async-done(((f32[2,4,128,128]{3,2,1,0:T(8,128)}, f32[2,128,128]{2,1,0:T(8,128)}), (f32[2,4,128,128]{3,2,1,0:T(8,128)}, f32[2,128,128]{2,1,0:T(8,128)})) %all-reduce.7.cloned.1.call-update) | async-done | bytes 655376 | tf_op jit(solution)/shard_map/psum | solution.py:359
  (402 shorter events, 230.8 us)
Async XLA Ops:
  7.2 56.4 %all-gather.3.cloned.1.call-start = ((), (), s32[]{:S(2)}) async-start(), calls=%async_computation.11 | async-start | bytes 1310720 | tf_op jit(solution)/shard_map/all_gather | solution.py:16
  10.7 116.6 %copy-start.56 = (f32[128]{0:T(128)}, f32[128]{0:T(128)S(1)}, u32[]{:S(2)}) copy-start(f32[128]{0:T(128)S(1)} %get-tuple-element.493) | copy-start | bytes 1540
  12.4 53.3 %copy-start.17 = (bf16[1,512,128]{2,1,0:T(8,128)(2,1)}, bf16[1,512,128]{2,1,0:T(8,128)(2,1)S(1)}, u32[]{:S(2)}) copy-start(bf16[1,512,128]{2,1,0:T(8,128)(2,1)S(1)} %fusion.128) | copy-start | bytes 393220
  19.2 44.3 %all-to-all-start = ((bf16[64,4,1,512]{3,1,2,0:T(4,128)(2,1)}), bf16[64,4,1,512]{3,1,2,0:T(4,128)(2,1)S(1)}, u32[]{:S(2)}, u32[]{:S(2)}) async-start(bf16[64,4,1,512]{3,1,2,0:T(4,128)(2,1)} %broadcast_in_dim.57), calls=%async_computation | async-start | bytes 524288 | tf_op jit(solution)/shard_map/all_to_all | solution.py:28
  39.8 134.6 %all-gather.5.cloned.1.call-start = ((), (), s32[]{:S(2)}) async-start(), calls=%async_computation.12 | async-start | bytes 1310720 | tf_op jit(solution)/shard_map/all_gather | solution.py:16
  134.3 8.6 all-to-all-start.4
  143.7 29.9 %all-to-all-start.3 = ((bf16[64,4,1,512]{3,1,2,0:T(4,128)(2,1)}), bf16[64,4,1,512]{3,1,2,0:T(4,128)(2,1)S(1)}, u32[]{:S(2)}, u32[]{:S(2)}) async-start(bf16[64,4,1,512]{3,1,2,0:T(4,128)(2,1)} %broadcast_in_dim.74), calls=%async_computation.3 | async-start | bytes 524288 | tf_op jit(solution)/shard_map/all_to_all | solution.py:28
  205.5 51.8 %copy-start.43 = (bf16[1,1,128,128]{2,3,1,0:T(8,128)(2,1)S(1)}, bf16[1,1,128,128]{2,3,1,0:T(8,128)(2,1)}, u32[]{:S(2)}) copy-start(bf16[1,1,128,128]{2,3,1,0:T(8,128)(2,1)} %copy-done.42) | copy-start | bytes 98308
  287.0 38.8 %all-to-all-start.6 = ((f32[64,4,1,512]{3,1,2,0:T(4,128)}), f32[64,4,1,512]{3,1,2,0:T(4,128)}, u32[]{:S(2)}, u32[]{:S(2)}) async-start(f32[64,4,1,512]{3,1,2,0:T(4,128)} %bitcast.128), calls=%async_computation.6 | async-start | bytes 1048576 | tf_op jit(solution)/shard_map/all_to_all | solution.py:49
  292.5 51.3 %copy-start.3 = (bf16[4,8,512,32]{2,3,1,0:T(8,128)(2,1)S(1)}, bf16[4,8,512,32]{2,3,1,0:T(8,128)(2,1)}, u32[]{:S(2)}) copy-start(bf16[4,8,512,32]{2,3,1,0:T(8,128)(2,1)} %get-tuple-element.225) | copy-start | bytes 3145732
  332.4 33.8 %all-to-all-start.7 = ((bf16[512,1,1,1,1,1,1,128]{7,6,5,4,3,2,1,0:T(2,128)(2,1)}), bf16[512,1,1,1,1,1,1,128]{7,6,5,4,3,2,1,0:T(2,128)(2,1)}, u32[]{:S(2)}, u32[]{:S(2)}) async-start(bf16[512,1,1,1,1,1,1,128]{7,6,5,4,3,2,1,0:T(2,128)(2,1)} %copy.171), calls=%async_computation.7 | async-start | bytes 524288 | tf_op jit(solution)/shard_map/all_to_all | solution.py:59
  369.2 8.6 all-to-all-start.8
  436.7 18.2 %all-to-all-start.9 = ((bf16[8,1,512,128]{3,2,1,0:T(8,128)(2,1)}), bf16[8,1,512,128]{3,2,1,0:T(8,128)(2,1)S(1)}, u32[]{:S(2)}, u32[]{:S(2)}) async-start(bf16[8,1,512,128]{3,2,1,0:T(8,128)(2,1)} %convert_bitcast_fusion), calls=%async_computation.9 | async-start | bytes 2097152 | tf_op jit(solution)/shard_map/all_to_all | solution.py:43
  454.8 99.2 %all-to-all-start.10 = ((f32[64,4,1,512]{3,1,2,0:T(4,128)}), f32[64,4,1,512]{3,1,2,0:T(4,128)S(1)}, u32[]{:S(2)}, u32[]{:S(2)}) async-start(f32[64,4,1,512]{3,1,2,0:T(4,128)} %bitcast.624), calls=%async_computation.10 | async-start | bytes 1048576 | tf_op jit(solution)/shard_map/all_to_all | solution.py:49
  461.7 92.1 %all-reduce.9.cloned.1.call-start = ((), (), s32[]{:S(2)}) async-start(), calls=%async_computation.14 | async-start | bytes 1310720 | tf_op jit(solution)/shard_map/psum | solution.py:355
  468.2 86.0 %copy-start.18 = (bf16[1,512,128]{2,1,0:T(8,128)(2,1)S(1)}, bf16[1,512,128]{2,1,0:T(8,128)(2,1)}, u32[]{:S(2)}) copy-start(bf16[1,512,128]{2,1,0:T(8,128)(2,1)} %copy-done.17) | copy-start | bytes 393220
  468.2 86.1 %copy-start.52 = (f32[512]{0:T(512)S(1)}, f32[512]{0:T(512)}, u32[]{:S(2)}) copy-start(f32[512]{0:T(512)} %copy-done.51) | copy-start | bytes 6148
  468.2 86.1 %copy-start.55 = (f32[128]{0:T(128)S(1)}, f32[128]{0:T(128)}, u32[]{:S(2)}) copy-start(f32[128]{0:T(128)} %copy-done.54) | copy-start | bytes 1540
  468.2 86.1 %copy-start.58 = (bf16[2,128,4]{1,2,0:T(4,128)(2,1)S(1)}, bf16[2,128,4]{1,2,0:T(4,128)(2,1)}, u32[]{:S(2)}) copy-start(bf16[2,128,4]{1,2,0:T(4,128)(2,1)} %param.25) | copy-start | bytes 6148
  469.1 85.8 %copy-start.60 = (f32[128]{0:T(128)S(1)}, f32[128]{0:T(128)}, u32[]{:S(2)}) copy-start(f32[128]{0:T(128)} %get-tuple-element.361) | copy-start | bytes 1540
  469.1 85.8 %copy-start.63 = (f32[128]{0:T(128)S(1)}, f32[128]{0:T(128)}, u32[]{:S(2)}) copy-start(f32[128]{0:T(128)} %get-tuple-element.355) | copy-start | bytes 1540
  469.1 241.1 %copy-start.13 = (f32[512,1,1,1,1,1,1,128]{7,6,5,4,3,2,1,0:T(1,128)S(1)}, f32[512,1,1,1,1,1,1,128]{7,6,5,4,3,2,1,0:T(1,128)}, u32[]{:S(2)}) copy-start(f32[512,1,1,1,1,1,1,128]{7,6,5,4,3,2,1,0:T(1,128)} %copy-done.12) | copy-start | bytes 786436
  469.1 241.1 %copy-start.28 = (bf16[1,512,128]{2,1,0:T(8,128)(2,1)S(1)}, bf16[1,512,128]{2,1,0:T(8,128)(2,1)}, u32[]{:S(2)}) copy-start(bf16[1,512,128]{2,1,0:T(8,128)(2,1)} %param.18) | copy-start | bytes 393220
  469.1 586.4 %all-reduce.7.cloned.1.call-start = ((), (), s32[]{:S(2)}) async-start(), calls=%async_computation.13 | async-start | bytes 1310720 | tf_op jit(solution)/shard_map/psum | solution.py:359
  (55 other events, 963.8 us)
Sparse Core Ops, SparseCore 0:
  17.7 35.9 all-gather.2
  133.8 18.4 all-gather.4
  469.2 84.5 all-reduce.8
  556.7 498.8 all-reduce.6
